TPU v7x, 128 devices: a whole 4x4x4 slice. The times are simulated.
128 devices in a mesh: replica: 1, data: 16 (over z, y), model: 8 (over x, core).
Axes of the slice: x: 4, y: 4, z: 4, core: 2. Of those that a mesh axis runs over, the one named last changes fastest.
Arguments:
- x_in: bfloat16 [32, 768, 2048], P(('replica', 'data'), 'model')
- lengths: int32 [32], P(('replica', 'data'))
- norm_gain: bfloat16 [2, 2048], P(None, 'data')
- w_in: bfloat16 [2, 2048, 34816], P(None, 'data', 'model')
- w_kv: bfloat16 [2, 2048, 512], P(None, 'data')
- w_out: bfloat16 [2, 18432, 2048], P(None, 'model', 'data')
Outputs:
- output: bfloat16 [32, 768, 2048], P(('replica', 'data'), 'model')
All inputs are finite; a program needn't handle non-finite values.
Results may differ from a plain program's by a relative error of at most 0.02.
Values are sent between devices in bfloat16 or wider.
A program may use at most 1 GiB of HBM per device.

v0:
```python
import jax
import jax.numpy as jnp
from jax import lax
from jax.sharding import PartitionSpec as P

EPS = 1e-6
NEG_BIG = -1e30


def layer_norm(hidden, norm_gain):
    values_f = hidden.astype(jnp.float32)
    row_mean = jnp.mean(values_f, axis=-1, keepdims=True)
    centered = values_f - row_mean
    row_var = jnp.mean(centered * centered, axis=-1, keepdims=True)
    return (centered * lax.rsqrt(row_var + EPS) * norm_gain.astype(jnp.float32)).astype(jnp.bfloat16)


def solution(mesh):
    batch_spec = ('replica', 'data')
    model_size = mesh.shape['model']

    def device_body(x_in, lengths, norm_gain, w_in, w_kv, w_out):
        batch_loc, seq_loc, model_width = x_in.shape
        head_dim = w_kv.shape[-1] // 2
        in_cols = w_in.shape[-1]
        out_rows = w_out.shape[1]
        ff_loc = in_cols - out_rows
        q_cols = out_rows - ff_loc
        heads_loc = q_cols // head_dim
        seq_len = seq_loc * model_size
        positions = jnp.arange(seq_len)
        causal = positions[None, :] <= positions[:, None]
        valid = positions[None, :] < lengths[:, None]
        allowed = causal[None, None, :, :] & valid[:, None, None, :]
        hidden = x_in
        for layer_idx in range(norm_gain.shape[0]):
            gain_full = lax.all_gather(norm_gain[layer_idx], 'data', axis=0, tiled=True)
            w_in_full = lax.all_gather(w_in[layer_idx], 'data', axis=0, tiled=True)
            w_kv_full = lax.all_gather(w_kv[layer_idx], 'data', axis=0, tiled=True)
            w_out_full = lax.all_gather(w_out[layer_idx], 'data', axis=1, tiled=True)
            normed = layer_norm(hidden, gain_full)
            normed_all = lax.all_gather(normed, 'model', axis=1, tiled=True)
            proj_out = jnp.einsum('btd,dc->btc', normed_all, w_in_full, preferred_element_type=jnp.float32).astype(jnp.bfloat16)
            kv_out = jnp.einsum('btd,dc->btc', normed_all, w_kv_full, preferred_element_type=jnp.float32).astype(jnp.bfloat16)
            queries = proj_out[:, :, :q_cols].reshape(batch_loc, seq_len, heads_loc, head_dim)
            scores = jnp.einsum('bthe,bse->bhts', queries, kv_out[:, :, :head_dim], preferred_element_type=jnp.float32) * head_dim ** -0.5
            scores = jnp.where(allowed, scores, NEG_BIG)
            attn_prob = jax.nn.softmax(scores, axis=-1)
            attn_out = jnp.einsum('bhts,bse->bthe', attn_prob, kv_out[:, :, head_dim:].astype(jnp.float32)).astype(jnp.bfloat16)
            gate_pre = proj_out[:, :, q_cols:q_cols + ff_loc].astype(jnp.float32)
            up_proj = proj_out[:, :, q_cols + ff_loc:].astype(jnp.float32)
            mlp_out = (jax.nn.silu(gate_pre) * up_proj).astype(jnp.bfloat16)
            joined = jnp.concatenate([attn_out.reshape(batch_loc, seq_len, q_cols), mlp_out], axis=-1)
            part_z = jnp.einsum('btr,rd->btd', joined, w_out_full, preferred_element_type=jnp.float32).astype(jnp.bfloat16)
            z_loc = lax.psum_scatter(part_z, 'model', scatter_dimension=1, tiled=True)
            hidden = (hidden.astype(jnp.float32) + z_loc.astype(jnp.float32)).astype(jnp.bfloat16)
        return hidden

    in_specs = (P(batch_spec, 'model', None), P(batch_spec), P(None, 'data'), P(None, 'data', 'model'), P(None, 'data', None), P(None, 'model', 'data'))
    return jax.shard_map(device_body, mesh=mesh, in_specs=in_specs, out_specs=P(batch_spec, 'model', None), check_vma=False)
```

profile of v0, /device:TPU:1, one launch (start us, length us, event | category | flops | bytes accessed | tf_op | source)
XLA Modules:
  0.0 725.1 jit_solution(12023520941883676343)
XLA Ops:
  6.5 1.9 fusion.113
  9.2 21.0 %all-gather = bf16[1,2048]{1,0:T(2,128)(2,1)S(1)} all-gather(bf16[1,128]{1,0:T(2,128)(2,1)S(1)} %get-tuple-element.14), channel_id=2, replica_groups=mesh['replica'=1,'data'=16,'model'=8] {'data'}, dimensions={1}, use_global_device_ids=true | all-gather | bytes 4352 | tf_op jit(solution)/shard_map/all_gather | solution.py:37
  30.2 1.4 convert_reduce_fusion.1
  31.6 1.5 fusion.79
  33.1 2.5 fusion.81
  35.7 1.5 fusion.111
  38.7 17.2 %all-gather.21.cloned.1.call-done = bf16[1,2048,512]{2,1,0:T(8,128)(2,1)} async-done(((bf16[1,128,512]{2,1,0:T(8,128)(2,1)}), bf16[1,2048,512]{2,1,0:T(8,128)(2,1)}) %all-gather.21.cloned.1.call-update) | async-done | bytes 2097168 | tf_op jit(solution)/shard_map/all_gather | solution.py:39
  56.0 43.7 %all-gather.17.cloned.1.call-done = bf16[2,768,2048]{2,1,0:T(8,128)(2,1)} async-done(((bf16[2,96,2048]{2,1,0:T(8,128)(2,1)}), bf16[2,768,2048]{2,1,0:T(8,128)(2,1)}) %all-gather.17.cloned.1.call-update) | async-done | bytes 6291472 | tf_op jit(solution)/shard_map/all_gather | solution.py:42
  99.7 6.8 fusion.70
  106.5 111.5 %all-gather.23.cloned.1.call-done = bf16[1,2048,4352]{2,1,0:T(8,128)(2,1)} async-done(((bf16[1,128,4352]{2,1,0:T(8,128)(2,1)}), bf16[1,2048,4352]{2,1,0:T(8,128)(2,1)}) %all-gather.23.cloned.1.call-update) | async-done | bytes 17825808 | tf_op jit(solution)/shard_map/all_gather | solution.py:38
  218.1 34.3 %fusion.14 = bf16[2,768,4352]{2,1,0:T(8,128)(2,1)S(1)} fusion(bf16[2,768,2048]{2,1,0:T(8,128)(2,1)} %all-gather.17.cloned.1.call-done, bf16[1,2048,4352]{2,1,0:T(8,128)(2,1)} %all-gather.23.cloned.1.call-done), kind=kOutput, calls=%fused_computation.18 | convolution fusion | flops 27387101184 | bytes 37486592 | tf_op jit(solution)/shard_map/btd,dc->btc/dot_general | solution.py:43
  253.6 1.5 fusion.46
  255.1 2.2 fusion.93
  257.3 5.3 fusion.13
  262.7 37.5 %all-gather.25.cloned.1.call-done = bf16[1,2304,2048]{2,1,0:T(8,128)(2,1)} async-done(((bf16[1,2304,128]{2,1,0:T(8,128)(2,1)}), bf16[1,2304,2048]{2,1,0:T(8,128)(2,1)}) %all-gather.25.cloned.1.call-update) | async-done | bytes 9437200 | tf_op jit(solution)/shard_map/all_gather | solution.py:40
  300.2 20.1 %fusion.36 = bf16[2,768,2048]{2,1,0:T(8,128)(2,1)} fusion(bf16[1,2304,2048]{2,1,0:T(8,128)(2,1)} %all-gather.25.cloned.1.call-done, bf16[2,768,2048]{2,1,0:T(8,128)(2,1)} %fusion.13, bf16[2,768,256]{2,1,0:T(8,128)(2,1)S(1)} %fusion.93), kind=kOutput, calls=%fused_computation.40 | convolution fusion | flops 14512816128 | bytes 22806528 | tf_op jit(solution)/shard_map/btr,rd->btd/dot_general | solution.py:54
  321.0 18.4 %all-gather.4 = bf16[1,2048]{1,0:T(2,128)(2,1)S(1)} all-gather(bf16[1,128]{1,0:T(2,128)(2,1)S(1)} %get-tuple-element.13), channel_id=6, replica_groups=mesh['replica'=1,'data'=16,'model'=8] {'data'}, dimensions={1}, use_global_device_ids=true | all-gather | bytes 4352 | tf_op jit(solution)/shard_map/all_gather | solution.py:37
  339.4 23.7 %reduce-scatter.3.cloned.1.call-done = bf16[2,96,2048]{2,1,0:T(8,128)(2,1)} async-done(((bf16[2,768,2048]{2,1,0:T(8,128)(2,1)}), bf16[2,96,2048]{2,1,0:T(8,128)(2,1)}) %reduce-scatter.3.cloned.1.call-update) | async-done | bytes 786448 | tf_op jit(solution)/shard_map/reduce_scatter | solution.py:55
  363.2 1.5 convert_reduce_fusion
  365.0 1.3 fusion.78
  367.9 40.7 %all-gather.27.cloned.1.call-done = bf16[1,2048,512]{2,1,0:T(8,128)(2,1)} async-done(((bf16[1,128,512]{2,1,0:T(8,128)(2,1)}), bf16[1,2048,512]{2,1,0:T(8,128)(2,1)}) %all-gather.27.cloned.1.call-update) | async-done | bytes 2097168 | tf_op jit(solution)/shard_map/all_gather | solution.py:39
  408.6 43.7 %all-gather.19.cloned.1.call-done = bf16[2,768,2048]{2,1,0:T(8,128)(2,1)} async-done(((bf16[2,96,2048]{2,1,0:T(8,128)(2,1)}), bf16[2,768,2048]{2,1,0:T(8,128)(2,1)}) %all-gather.19.cloned.1.call-update) | async-done | bytes 6291472 | tf_op jit(solution)/shard_map/all_gather | solution.py:42
  452.3 8.0 %fusion.73 = bf16[2,768,512]{2,1,0:T(8,128)(2,1)} fusion(bf16[2,768,2048]{2,1,0:T(8,128)(2,1)} %all-gather.19.cloned.1.call-done, bf16[1,2048,512]{2,1,0:T(8,128)(2,1)} %all-gather.27.cloned.1.call-done), kind=kOutput, calls=%fused_computation.74 | convolution fusion | flops 3222011904 | bytes 9961472 | tf_op jit(solution)/shard_map/btd,dc->btc/dot_general | solution.py:44
  460.4 110.3 %all-gather.29.cloned.1.call-done = bf16[1,2048,4352]{2,1,0:T(8,128)(2,1)} async-done(((bf16[1,128,4352]{2,1,0:T(8,128)(2,1)}), bf16[1,2048,4352]{2,1,0:T(8,128)(2,1)}) %all-gather.29.cloned.1.call-update) | async-done | bytes 17825808 | tf_op jit(solution)/shard_map/all_gather | solution.py:38
  570.7 34.4 %fusion.17 = bf16[2,768,4352]{2,1,0:T(8,128)(2,1)S(1)} fusion(bf16[2,768,2048]{2,1,0:T(8,128)(2,1)} %all-gather.19.cloned.1.call-done, bf16[1,2048,4352]{2,1,0:T(8,128)(2,1)} %all-gather.29.cloned.1.call-done), kind=kOutput, calls=%fused_computation.19 | convolution fusion | flops 27387101184 | bytes 37486592 | tf_op jit(solution)/shard_map/btd,dc->btc/dot_general | solution.py:43
  606.4 1.5 fusion.47
  607.8 2.2 fusion.90
  610.1 5.2 fusion.12
  615.3 37.7 %all-gather.31.cloned.1.call-done = bf16[1,2304,2048]{2,1,0:T(8,128)(2,1)} async-done(((bf16[1,2304,128]{2,1,0:T(8,128)(2,1)}), bf16[1,2304,2048]{2,1,0:T(8,128)(2,1)}) %all-gather.31.cloned.1.call-update) | async-done | bytes 9437200 | tf_op jit(solution)/shard_map/all_gather | solution.py:40
  652.9 20.2 %fusion.41 = bf16[2,768,2048]{2,1,0:T(8,128)(2,1)} fusion(bf16[1,2304,2048]{2,1,0:T(8,128)(2,1)} %all-gather.31.cloned.1.call-done, bf16[2,768,2048]{2,1,0:T(8,128)(2,1)} %fusion.12, bf16[2,768,256]{2,1,0:T(8,128)(2,1)S(1)} %fusion.90), kind=kOutput, calls=%fused_computation.41 | convolution fusion | flops 14512816128 | bytes 22806528 | tf_op jit(solution)/shard_map/btr,rd->btd/dot_general | solution.py:54
  673.2 42.8 %reduce-scatter.5.cloned.1.call-done = bf16[2,96,2048]{2,1,0:T(8,128)(2,1)} async-done(((bf16[2,768,2048]{2,1,0:T(8,128)(2,1)}), bf16[2,96,2048]{2,1,0:T(8,128)(2,1)}) %reduce-scatter.5.cloned.1.call-update) | async-done | bytes 786448 | tf_op jit(solution)/shard_map/reduce_scatter | solution.py:55
  716.0 2.3 fusion.83
  (43 shorter events, 7.3 us)
Async XLA Ops:
  6.5 29.2 %copy-start.1 = (bf16[2,128,4352]{2,1,0:T(8,128)(2,1)S(1)}, bf16[2,128,4352]{2,1,0:T(8,128)(2,1)}, u32[]{:S(2)}) copy-start(bf16[2,128,4352]{2,1,0:T(8,128)(2,1)} %param.9) | copy-start | bytes 6684676
  6.5 49.4 %all-gather.21.cloned.1.call-start = ((), (), s32[]{:S(2)}) async-start(), calls=%async_computation.6 | async-start | bytes 2228224 | tf_op jit(solution)/shard_map/all_gather | solution.py:39
  8.4 91.3 %all-gather.17.cloned.1.call-start = ((), (), s32[]{:S(2)}) async-start(), calls=%async_computation.2 | async-start | bytes 7077888 | tf_op jit(solution)/shard_map/all_gather | solution.py:42
  30.2 7.1 copy-start.2
  35.6 3.0 copy-start.3
  35.6 182.4 %all-gather.23.cloned.1.call-start = ((), (), s32[]{:S(2)}) async-start(), calls=%async_computation.7 | async-start | bytes 18939904 | tf_op jit(solution)/shard_map/all_gather | solution.py:38
  37.2 262.9 %all-gather.25.cloned.1.call-start = ((), (), s32[]{:S(2)}) async-start(), calls=%async_computation.8 | async-start | bytes 10027008 | tf_op jit(solution)/shard_map/all_gather | solution.py:40
  38.4 324.7 %reduce-scatter.3.cloned.1.call-start = ((), (), s32[]{:S(2)}) async-start(), calls=%async_computation.3 | async-start | bytes 7077888 | tf_op jit(solution)/shard_map/reduce_scatter | solution.py:55
  320.3 42.9 %copy-start = (bf16[2,96,2048]{2,1,0:T(8,128)(2,1)S(1)}, bf16[2,96,2048]{2,1,0:T(8,128)(2,1)}, u32[]{:S(2)}) copy-start(bf16[2,96,2048]{2,1,0:T(8,128)(2,1)} %param.6) | copy-start | bytes 2359300
  320.3 88.3 %all-gather.27.cloned.1.call-start = ((), (), s32[]{:S(2)}) async-start(), calls=%async_computation.9 | async-start | bytes 2228224 | tf_op jit(solution)/shard_map/all_gather | solution.py:39
  320.9 131.4 %all-gather.19.cloned.1.call-start = ((), (), s32[]{:S(2)}) async-start(), calls=%async_computation.4 | async-start | bytes 7077888 | tf_op jit(solution)/shard_map/all_gather | solution.py:42
  366.4 204.3 %all-gather.29.cloned.1.call-start = ((), (), s32[]{:S(2)}) async-start(), calls=%async_computation.10 | async-start | bytes 18939904 | tf_op jit(solution)/shard_map/all_gather | solution.py:38
  367.1 285.8 %all-gather.31.cloned.1.call-start = ((), (), s32[]{:S(2)}) async-start(), calls=%async_computation.11 | async-start | bytes 10027008 | tf_op jit(solution)/shard_map/all_gather | solution.py:40
  367.8 348.2 %reduce-scatter.5.cloned.1.call-start = ((), (), s32[]{:S(2)}) async-start(), calls=%async_computation.5 | async-start | bytes 7077888 | tf_op jit(solution)/shard_map/reduce_scatter | solution.py:55
  570.7 34.4 %copy-start.4 = (bf16[2,768,512]{2,1,0:T(8,128)(2,1)S(1)}, bf16[2,768,512]{2,1,0:T(8,128)(2,1)}, u32[]{:S(2)}) copy-start(bf16[2,768,512]{2,1,0:T(8,128)(2,1)} %fusion.73) | copy-start | bytes 4718596
Sparse Core Ops, SparseCore 0:
  9.5 46.4 all-gather.20
  57.7 41.9 all-gather.16
  101.8 116.1 all-gather.22
  220.0 80.0 all-gather.24
  320.5 42.6 reduce-scatter.2
  365.2 43.4 all-gather.26
  410.3 41.9 all-gather.18
  454.5 116.1 all-gather.28
  572.8 80.0 all-gather.30
  673.3 42.6 reduce-scatter.4
where the time goes:
time: 725 us
  waiting for transfers between devices  511 us (70%)
  matrix products  131 us (18%)
  blocking collectives  39.4 us (5%)
  other arithmetic  24.7 us (3%)
  between operations  13.7 us (2%)
    all_gather x2, waiting for transfers between devices, device_body(): w_in_full = lax.all_gather(w_in[layer_idx], 'data', axis=0, tiled=True)  222 us
    all_gather x2, waiting for transfers between devices, device_body(): normed_all = lax.all_gather(normed, 'model', axis=1, tiled=True)  87.4 us
    all_gather x2, waiting for transfers between devices, device_body(): w_out_full = lax.all_gather(w_out[layer_idx], 'data', axis=1, tiled=True)  75.2 us
    dot_general x2, matrix products, device_body(): jnp.einsum('btd,dc->btc', normed_all, w_in_full, preferred_element_type=j...  68.7 us
    reduce_scatter x2, waiting for transfers between devices, device_body(): z_loc = lax.psum_scatter(part_z, 'model', scatter_dimension=1, tiled=True)  66.6 us
    all_gather x2, waiting for transfers between devices, device_body(): w_kv_full = lax.all_gather(w_kv[layer_idx], 'data', axis=0, tiled=True)  58 us
    dot_general x2, matrix products, device_body(): jnp.einsum('btr,rd->btd', joined, w_out_full, preferred_element_type=jnp....  40.4 us
    all_gather x2, blocking collectives, device_body(): gain_full = lax.all_gather(norm_gain[layer_idx], 'data', axis=0, tiled=True)  39.4 us
  transfers between devices with their start and end apart: 10, of which 10 were waited for; matrix products, arithmetic and copies ran while one was open for 16% of the time, Pallas kernels for 0%

commit v1 on v0

v1 whole, which is shorter than its diff:
```python
import jax
import jax.numpy as jnp
from jax import lax
from jax.experimental import pallas as pl
from jax.experimental.pallas import tpu as pltpu
from jax.sharding import PartitionSpec as P

EPS = 1e-6
NEG_BIG = -1e30
MESH = pl.DeviceIdType.MESH
TILE = 512
RELS = (0, -1, 1, 2)
GROUPS = ((0, 'in'), (0, 'out'), (1, 'in'), (1, 'out'))
F32 = jnp.float32
BF16 = jnp.bfloat16
ORDER = ((0, 1), (4, 8), (2, 3), (5, 9), (6, 10), (7, 11), (12, 13), (14, 15))


def dot(a, b):
    return jnp.dot(a, b, preferred_element_type=F32)


def layer_kernel(ring, x_ref, gain_ref, valid_ref, win_ref, wout_ref, y_ref, winb, woutb,
                 h_all, joined, kvb, qb, wt, wo, zp, zrp, xh, xf, zs, hid, gbuf,
                 gsend, grecv, wsend, wrecv, asend, arecv, rsend, rrecv, bsem, tsem, osem):
    batch, blk, width = x_ref.shape
    shard = win_ref.shape[1]
    in_cols = win_ref.shape[2]
    out_rows = wout_ref.shape[1]
    head = qb.shape[-1]
    seq = h_all.shape[1]
    n_data = gbuf.shape[0]
    me = lax.axis_index('data')
    mi = lax.axis_index('model')
    yy = lax.rem(me, ring)
    zz = lax.div(me, ring)
    xx = lax.div(mi, 2)
    cc = lax.rem(mi, 2)

    def wrap(value, rel):
        return lax.rem(value + (rel + ring), ring)

    def data_at(ry, rz):
        return wrap(zz, rz) * ring + wrap(yy, ry)

    def dev_data(ry, rz):
        return {'data': data_at(ry, rz), 'model': mi}

    def dev_x(rx):
        return {'data': me, 'model': wrap(xx, rx) * 2 + cc}

    partner = {'data': me, 'model': xx * 2 + (1 - cc)}

    barrier = pltpu.get_barrier_semaphore()
    for ry in range(ring):
        for rz in range(ring):
            if ry or rz:
                pl.semaphore_signal(barrier, inc=1, device_id=dev_data(ry, rz), device_id_type=MESH)
    for dev in (dev_x(1), dev_x(-1), partner):
        pl.semaphore_signal(barrier, inc=1, device_id=dev, device_id_type=MESH)
    pl.semaphore_wait(barrier, n_data - 1 + 3)

    drains = []

    def remote(src, dst, ssem, rsem, dev):
        return pltpu.make_async_remote_copy(src_ref=src, dst_ref=dst, send_sem=ssem, recv_sem=rsem,
                                            device_id=dev, device_id_type=MESH)

    half_cols = in_cols // 2
    half_rows = out_rows // 2

    def unit(g, hf, rp, rq, part=None):
        layer, kind = GROUPS[g]
        s = data_at(rp, rq) if hf == 0 else data_at(rq, rp)
        if kind == 'in':
            n = shard if part is None else shard // 2
            start = pl.multiple_of(s * shard + (0 if part is None else part * n), 64)
            return winb.at[layer, pl.ds(start, n), pl.ds(hf * half_cols, half_cols)]
        n = half_rows if part is None else half_rows // 2
        return woutb.at[layer, s, pl.ds(hf * half_rows + (0 if part is None else part * n), n), :]

    def own(g, hf):
        layer, kind = GROUPS[g]
        if kind == 'in':
            return win_ref.at[layer, :, pl.ds(hf * half_cols, half_cols)]
        return wout_ref.at[layer, pl.ds(hf * half_rows, half_rows), :]

    def along(hf, primary, rel):
        on_y = (hf == 0) == primary
        return dev_data(rel, 0) if on_y else dev_data(0, rel)

    def send(g, hf, idx, rel, primary, to, part=None):
        def build():
            dst = unit(g, hf, rel[0], rel[1], part)
            src = own(g, hf) if rel == (0, 0) else dst
            return remote(src, dst, wsend.at[g, hf, idx], wrecv.at[g, hf, idx], along(hf, primary, to))
        build().start()
        drains.append(build)

    def spec(idx):
        if idx < 4:
            return ((-1, 0, None), (1, 0, None), (2, 0, 0), (2, 0, 1))[idx]
        return (RELS[idx % 4], (None, -1, 1, 2)[idx // 4], None)

    def start_group(g):
        for hf in (0, 1):
            send(g, hf, 0, (0, 0), True, 1)
            send(g, hf, 1, (0, 0), True, -1)
        for hf in (0, 1):
            send(g, hf, 4, (0, 0), False, 1)
            send(g, hf, 8, (0, 0), False, -1)

    def arrive(g, hf, idx):
        rp, rq, part = spec(idx)
        ref = unit(g, hf, rp, rq, part)
        remote(ref, ref, wsend.at[g, hf, idx], wrecv.at[g, hf, idx], along(hf, True, 1)).wait_recv()
        if idx == 0:
            send(g, hf, 2, (-1, 0), True, 1, 0)
            send(g, hf, 5, (-1, 0), False, 1)
            send(g, hf, 9, (-1, 0), False, -1)
        elif idx == 1:
            send(g, hf, 3, (1, 0), True, -1, 1)
            send(g, hf, 6, (1, 0), False, 1)
            send(g, hf, 10, (1, 0), False, -1)
        elif idx == 3:
            send(g, hf, 7, (2, 0), False, 1)
            send(g, hf, 11, (2, 0), False, -1)
        elif idx == 4:
            send(g, hf, 12, (0, -1), False, 1)
        elif idx == 5:
            send(g, hf, 13, (-1, -1), False, 1)
        elif idx == 10:
            send(g, hf, 14, (1, 1), False, -1)
        elif idx == 11:
            send(g, hf, 15, (2, 1), False, -1)

    events = []
    for g in range(len(GROUPS)):
        count = 0
        for pair in ORDER:
            for hf in (0, 1):
                for idx in pair:
                    if count == 24 and g + 1 < len(GROUPS):
                        events.append((g, lambda g=g: start_group(g + 1)))
                    events.append((g, lambda g=g, hf=hf, idx=idx: arrive(g, hf, idx)))
                    count += 1
    cursor = [0]

    def pump(n):
        for _ in range(n):
            if cursor[0] < len(events):
                events[cursor[0]][1]()
                cursor[0] += 1

    def pump_group(g):
        while cursor[0] < len(events) and events[cursor[0]][0] <= g:
            pump(1)

    gain_copies = []
    for ry in range(ring):
        for rz in range(ring):
            if ry or rz:
                k = rz * ring + ry
                copy = remote(gain_ref, gbuf.at[me], gsend.at[k], grecv.at[k], dev_data(ry, rz))
                copy.start()
                gain_copies.append((k, ry, rz))
    start_group(0)
    locals_ = []
    for layer in (0, 1):
        locals_.append(pltpu.make_async_copy(win_ref.at[layer], winb.at[layer, pl.ds(pl.multiple_of(me * shard, 128), shard), :], bsem.at[layer, 0]))
        locals_.append(pltpu.make_async_copy(wout_ref.at[layer], woutb.at[layer, me], bsem.at[layer, 1]))
    for copy in locals_:
        copy.start()
    hid[...] = x_ref[...]
    gbuf[me] = gain_ref[...]
    for k, ry, rz in gain_copies:
        src = gbuf.at[data_at(-ry, -rz)]
        remote(gain_ref, src, gsend.at[k], grecv.at[k], partner).wait()
    for copy in locals_:
        copy.wait()

    def block(rx, core, b=None):
        rows = pl.ds(pl.multiple_of((wrap(xx, rx) * 2 + core) * blk, 32), blk)
        return h_all.at[:, rows, :] if b is None else h_all.at[b, rows, :]

    def a_send(layer, idx, ref, dev, out):
        copy = remote(ref, ref, asend.at[layer, idx], arecv.at[layer, idx], dev)
        copy.start()
        out.append(copy)

    def a_wait(layer, idx, ref):
        remote(ref, ref, asend.at[layer, idx], arecv.at[layer, idx], partner).wait_recv()

    def norm_and_send(layer, out):
        rows = pl.ds(pl.multiple_of(mi * blk, 32), blk)
        for b in range(batch):
            values = hid[b].astype(F32)
            centered = values - jnp.mean(values, axis=-1, keepdims=True)
            var = jnp.mean(centered * centered, axis=-1, keepdims=True)
            normed = centered * lax.rsqrt(var + EPS)
            for i in range(n_data):
                cols = slice(i * shard, (i + 1) * shard)
                h_all[b, rows, cols] = (normed[:, cols] * gbuf[i, layer:layer + 1, :]).astype(BF16)
        mine = block(0, cc)
        a_send(layer, 0, mine, dev_x(1), out)
        a_send(layer, 1, mine, dev_x(-1), out)
        a_send(layer, 4, mine, partner, out)

    def gather_near(layer, out):
        a_wait(layer, 0, block(-1, cc))
        a_send(layer, 2, block(-1, cc, 0), dev_x(1), out)
        a_send(layer, 5, block(-1, cc), partner, out)
        a_wait(layer, 1, block(1, cc))
        a_send(layer, 3, block(1, cc, 1), dev_x(-1), out)
        a_send(layer, 6, block(1, cc), partner, out)

    def gather_far(layer, out):
        a_wait(layer, 2, block(2, cc, 0))
        a_send(layer, 7, block(2, cc, 0), partner, out)
        a_wait(layer, 3, block(2, cc, 1))
        a_send(layer, 8, block(2, cc, 1), partner, out)

    def gather_rest(layer):
        a_wait(layer, 4, block(0, 1 - cc))
        a_wait(layer, 5, block(-1, 1 - cc))
        a_wait(layer, 6, block(1, 1 - cc))
        a_wait(layer, 7, block(2, 1 - cc, 0))
        a_wait(layer, 8, block(2, 1 - cc, 1))

    n_mlp = (in_cols - 3 * head) // TILE
    m_rows = seq // 2

    def w_tile(layer, t, slot):
        return pltpu.make_async_copy(winb.at[layer, :, pl.ds(pl.multiple_of(t * TILE, TILE), TILE)], wt.at[slot], tsem.at[slot])

    def q_tile(layer, slot):
        return pltpu.make_async_copy(winb.at[layer, :, pl.ds((n_mlp + 1) * TILE, head)], wt.at[slot, :, pl.ds(0, head)], tsem.at[slot])

    def over_rows(fn):
        def body(i, carry):
            b = lax.div(i, 2)
            rows = pl.ds(pl.multiple_of(lax.rem(i, 2) * m_rows, m_rows), m_rows)
            fn(b, rows)
            return carry
        lax.fori_loop(0, 2 * batch, body, 0)

    def in_proj(layer, pumps):
        w_tile(layer, n_mlp, 0).start()
        q_tile(layer, 1).start()
        w_tile(layer, n_mlp, 0).wait()

        def do_kv(b, rows):
            kvb[b, rows, :] = dot(h_all[b, rows, :], wt[0]).astype(BF16)

        def do_q(b, rows):
            qb[b, rows, :] = dot(h_all[b, rows, :], wt[1, :, :head]).astype(BF16)

        over_rows(do_kv)
        w_tile(layer, 0, 0).start()
        pump(pumps)
        q_tile(layer, 1).wait()
        over_rows(do_q)
        pump(pumps)
        w_tile(layer, 1, 1).start()

        def body(t, carry):
            slot = lax.rem(t, 2)
            w_tile(layer, t, slot).wait()

            def do_mlp(b, rows):
                res = dot(h_all[b, rows, :], wt[slot])
                gate = res[:, :head].astype(BF16).astype(F32)
                up = res[:, head:].astype(BF16).astype(F32)
                cols = pl.ds(pl.multiple_of(head + t * head, head), head)
                joined[b, rows, cols] = (gate * jax.nn.sigmoid(gate) * up).astype(BF16)

            over_rows(do_mlp)

            @pl.when(t + 2 < n_mlp)
            def _():
                w_tile(layer, t + 2, slot).start()

            for k in range(n_mlp):
                @pl.when(t == k)
                def _():
                    pump(pumps)
            return carry

        lax.fori_loop(0, n_mlp, body, 0)

    def wo_copy(layer, s):
        return pltpu.make_async_copy(woutb.at[layer, s], wo.at[:, pl.ds(s * shard, shard)], osem.at[s])

    q_rows = 256

    def attention():
        def body(b, carry):
            for m in range(seq // q_rows):
                keys = (m + 1) * q_rows
                q = qb[b, m * q_rows:(m + 1) * q_rows, :]
                k = kvb[b, :keys, :head]
                s = lax.dot_general(q, k, (((1,), (1,)), ((), ())), preferred_element_type=F32) * head ** -0.5
                row = lax.broadcasted_iota(jnp.int32, (q_rows, keys), 0) + m * q_rows
                col = lax.broadcasted_iota(jnp.int32, (q_rows, keys), 1)
                allowed = (col <= row) & (valid_ref[b, :, :keys] > 0.5)
                s = jnp.where(allowed, s, NEG_BIG)
                e = jnp.exp(s - jnp.max(s, axis=-1, keepdims=True))
                p = e / jnp.sum(e, axis=-1, keepdims=True)
                o = dot(p, kvb[b, :keys, head:].astype(F32))
                joined[b, m * q_rows:(m + 1) * q_rows, :head] = o.astype(BF16)
            return carry
        lax.fori_loop(0, batch, body, 0)

    PAIRS = (2, 1, -1, 0)
    pair_rows = 2 * blk

    def out_proj(p):
        rows = pl.ds(pl.multiple_of(wrap(xx, PAIRS[p]) * pair_rows, 64), pair_rows)

        def body(n, carry):
            cols = pl.ds(pl.multiple_of(n * TILE, TILE), TILE)
            lhs = joined[:, rows, :].reshape(batch * pair_rows, out_rows)
            res = dot(lhs, wo[:, cols]).astype(BF16)
            zp[p, :, :, cols] = res.reshape(batch, pair_rows, TILE)
            return carry
        lax.fori_loop(0, width // TILE, body, 0)

    mine_rows = pl.ds(pl.multiple_of(cc * blk, 32), blk)
    other_rows = pl.ds(pl.multiple_of((1 - cc) * blk, 32), blk)

    def reduce_scatter(layer, out_ref, pumps):
        sends = []

        def r_send(idx, src, dst, dev):
            copy = remote(src, dst, rsend.at[layer, idx], rrecv.at[layer, idx], dev)
            copy.start()
            sends.append(copy)

        def r_wait(idx, dst):
            remote(dst, dst, rsend.at[layer, idx], rrecv.at[layer, idx], partner).wait_recv()

        def chunks(fn):
            for b in range(batch):
                def body(n, carry):
                    fn(b, pl.ds(pl.multiple_of(n * TILE, TILE), TILE))
                    return carry
                lax.fori_loop(0, width // TILE, body, 0)

        def base(p, b, cols):
            return zp[p, b, mine_rows, cols].astype(F32) + zrp[p, b, :, cols].astype(F32)

        def finish(p):
            r_wait(p, zrp.at[p])
            if p == 0:
                def fn(b, cols):
                    zs[0, b, :, cols] = base(0, b, cols).astype(BF16)
                chunks(fn)
                r_send(4, zs.at[0, 0], xh.at[0], dev_x(1))
                r_send(5, zs.at[0, 1], xh.at[1], dev_x(-1))
            elif p < 3:
                r_wait(3 + p, xh.at[p - 1])

                def fn(b, cols):
                    total = base(p, b, cols)
                    if b == p - 1:
                        total = total + xh[p - 1, :, cols].astype(F32)
                    zs[p, b, :, cols] = total.astype(BF16)
                chunks(fn)
                r_send(5 + p, zs.at[p], xf.at[p - 1], dev_x(1 if p == 1 else -1))
            else:
                r_wait(6, xf.at[0])
                r_wait(7, xf.at[1])

                def fn(b, cols):
                    total = base(3, b, cols) + xf[0, b, :, cols].astype(F32) + xf[1, b, :, cols].astype(F32)
                    out_ref[b, :, cols] = (hid[b, :, cols].astype(F32) + total).astype(BF16)
                chunks(fn)

        for p in range(4):
            out_proj(p)
            r_send(p, zp.at[p, :, other_rows, :], zrp.at[p], partner)
            pump(pumps)
            if p:
                finish(p - 1)
        pump(2 * pumps)
        finish(3)
        for copy in sends:
            copy.wait_send()

    for layer in (0, 1):
        a_sends = []
        norm_and_send(layer, a_sends)
        pump(8 if layer == 0 else 4)
        gather_near(layer, a_sends)
        pump(4)
        gather_far(layer, a_sends)
        pump(2)
        gather_rest(layer)
        pump_group(2 * layer)
        in_proj(layer, 3)
        for copy in a_sends:
            copy.wait_send()
        attention()
        pump_group(2 * layer + 1)
        for s in range(n_data):
            wo_copy(layer, s).start()
        for s in range(n_data):
            wo_copy(layer, s).wait()
        reduce_scatter(layer, hid if layer == 0 else y_ref, 2)

    for build in drains:
        build().wait_send()


def solution(mesh):
    batch_spec = ('replica', 'data')
    model_size = mesh.shape['model']
    n_data = mesh.shape['data']
    ring = 4
    assert model_size == 2 * ring and n_data == ring * ring

    def device_body(x_in, lengths, norm_gain, w_in, w_kv, w_out):
        batch, blk, width = x_in.shape
        layers, shard, in_cols = w_in.shape
        out_rows = w_out.shape[1]
        head = w_kv.shape[-1] // 2
        ff = in_cols - out_rows
        seq = blk * model_size
        valid = (jnp.arange(seq)[None, None, :] < lengths[:, None, None]).astype(F32)
        gain = jnp.zeros((8, shard), F32).at[:layers].set(norm_gain.astype(F32))
        gate = w_in[:, :, head:head + ff].reshape(layers, shard, ff // head, 1, head)
        up = w_in[:, :, head + ff:].reshape(layers, shard, ff // head, 1, head)
        gate_up = jnp.concatenate([gate, up], axis=3).reshape(layers, shard, 2 * ff)
        win = jnp.concatenate([gate_up, w_kv, w_in[:, :, :head]], axis=-1)
        total = win.shape[-1]
        vmem = pl.BlockSpec(memory_space=pltpu.VMEM)
        hbm = pl.BlockSpec(memory_space=pl.ANY)
        dma = pltpu.SemaphoreType.DMA
        y, _, _ = pl.pallas_call(
            lambda *refs: layer_kernel(ring, *refs),
            name='layers',
            out_shape=(
                jax.ShapeDtypeStruct(x_in.shape, BF16),
                jax.ShapeDtypeStruct((layers, width, total), BF16),
                jax.ShapeDtypeStruct((layers, n_data, out_rows, shard), BF16),
            ),
            in_specs=[vmem] * 5,
            out_specs=(vmem, hbm, hbm),
            scratch_shapes=[
                pltpu.VMEM((batch, seq, width), BF16),
                pltpu.VMEM((batch, seq, out_rows), BF16),
                pltpu.VMEM((batch, seq, 2 * head), BF16),
                pltpu.VMEM((batch, seq, head), BF16),
                pltpu.VMEM((2, width, TILE), BF16),
                pltpu.VMEM((out_rows, width), BF16),
                pltpu.VMEM((4, batch, 2 * blk, width), BF16),
                pltpu.VMEM((4, batch, blk, width), BF16),
                pltpu.VMEM((2, blk, width), BF16),
                pltpu.VMEM((2, batch, blk, width), BF16),
                pltpu.VMEM((3, batch, blk, width), BF16),
                pltpu.VMEM((batch, blk, width), BF16),
                pltpu.VMEM((n_data, 8, shard), F32),
                dma((n_data,)), dma((n_data,)),
                dma((4, 2, 16)), dma((4, 2, 16)),
                dma((2, 9)), dma((2, 9)),
                dma((2, 8)), dma((2, 8)),
                dma((2, 2)), dma((2,)), dma((n_data,)),
            ],
            compiler_params=pltpu.CompilerParams(
                collective_id=0, has_side_effects=True, vmem_limit_bytes=67043328),
            cost_estimate=pl.CostEstimate(flops=95_000_000_000, bytes_accessed=200_000_000, transcendentals=0),
        )(x_in, gain, valid, win, w_out)
        return y

    in_specs = (P(batch_spec, 'model', None), P(batch_spec), P(None, 'data'), P(None, 'data', 'model'), P(None, 'data', None), P(None, 'model', 'data'))
    return jax.shard_map(device_body, mesh=mesh, in_specs=in_specs, out_specs=P(batch_spec, 'model', None), check_vma=False)
```

time: 725 us -> 402 us (0.55)
  waiting for transfers between devices: 511 us -> 0 us
  Pallas kernels: 0 us -> 371 us
  matrix products: 131 us -> 0 us
  blocking collectives: 39.4 us -> 0 us
  other arithmetic: 24.7 us -> 10.9 us
  between operations: 13.7 us -> 0.05 us
  local copies, waits for them, and re-layouts: 5.24 us -> 16.7 us
    all_gather x8 -> x0, waiting for transfers between devices: 442 us -> none  [the longest x2 222 us: device_body(): w_in_full = lax.all_gather(w_in[layer_idx], 'data', axis=0, tiled=True)]
    pallas_call x0 -> x1, Pallas kernels: none -> 371 us  [device_body(): pl.pallas_call(lambda *refs: layer_kernel(ring, *refs), name='layers', ou...]
    dot_general x10 -> x0, matrix products: 131 us -> none  [the longest x2 68.7 us: device_body(): jnp.einsum('btd,dc->btc', normed_all, w_in_full, preferred_element_type=j...]
    reduce_scatter x2 -> x0, waiting for transfers between devices: 66.6 us -> none  [device_body(): z_loc = lax.psum_scatter(part_z, 'model', scatter_dimension=1, tiled=True)]
    all_gather x2 -> x0, blocking collectives: 39.4 us -> none  [device_body(): gain_full = lax.all_gather(norm_gain[layer_idx], 'data', axis=0, tiled=True)]
    convert_element_type x7 -> x1, other arithmetic: 16.7 us -> 1.32 us  [device_body(): (jnp.arange(seq)[None, None, :] < lengths[:, None, None]).astype(F32)]
    reshape x0 -> x3, local copies, waits for them, and re-layouts: none -> 11.9 us  [the longest x1 4.72 us: device_body(): w_in[:, :, head:head + ff].reshape(layers, shard, ff // head, 1, head)]
    concatenate x0 -> x2, other arithmetic: none -> 8.34 us  [the longest x1 6.67 us: device_body(): gate_up = jnp.concatenate([gate, up], axis=3).reshape(layers, shard, 2 * ff)]
  transfers between devices with their start and end apart: 10 -> 0, of which waited for: 10 -> 0; matrix products, arithmetic and copies ran while one was open for 16% -> 0% of each run, Pallas kernels for 0% -> 0%
where the time goes in v1:
time: 402 us; the launch traced here: 399 us
  Pallas kernels  371 us (92%)
  local copies, waits for them, and re-layouts  16.7 us (4%)
  other arithmetic  10.9 us (3%)
    pallas_call x1, Pallas kernels, device_body(): pl.pallas_call(lambda *refs: layer_kernel(ring, *refs), name='layers', ou...  371 us

profile of v1, /device:TPU:1, one launch (start us, length us, event | category | flops | bytes accessed | tf_op | source)
XLA Modules:
  0.0 398.9 jit_solution(15719117427033966857)
XLA Ops:
  0.0 1.3 pad_convert_fusion.refs_1_
  1.3 1.3 compare_convert_fusion.refs_2_
  2.6 2.7 fusion
  5.3 4.7 %reshape.73 = bf16[2,128,8,1,256]{4,3,2,1,0:T(2,128)(2,1)S(1)} reshape(bf16[2,128,2048]{2,1,0:T(8,128)(2,1)} %get-tuple-element.19) | data formatting | bytes 2097152 | tf_op jit(solution)/shard_map/reshape | solution.py:431
  10.0 3.9 reshape.74
  13.9 6.7 %pad_maximum_fusion.1 = bf16[2,128,8,2,256]{4,3,2,1,0:T(2,128)(2,1)} fusion(bf16[2,128,8,1,256]{4,3,2,1,0:T(2,128)(2,1)} %reshape.74, bf16[2,128,8,1,256]{4,3,2,1,0:T(2,128)(2,1)S(1)} %reshape.73), kind=kLoop, calls=%fused_computation.1 | loop fusion | flops 4194304 | bytes 4194304 | tf_op jit(solution)/shard_map/concatenate | solution.py:433
  20.6 0.0 slice-start
  20.6 0.0 copy-start
  20.6 3.3 reshape.72
  23.9 0.0 slice-done
  23.9 0.0 copy-done
  23.9 1.7 pad_maximum_fusion.refs_3_
  25.6 371.2 %layers.1 = (bf16[2,96,2048]{2,1,0:T(8,128)(2,1)}, bf16[2,2048,4864]{2,1,0:T(8,128)(2,1)}, bf16[2,16,2304,128]{3,2,1,0:T(8,128)(2,1)}) custom-call(bf16[2,96,2048]{2,1,0:T(8,128)(2,1)} %refs_0_.1, f32[8,128]{1,0:T(8,128)} %pad_convert_fusion.refs_1_, f32[2,1,768]{2,1,0:T(1,128)} %compare_convert_fusion.refs_2_, ...), custom_call_target="tpu_custom_call" | custom-call | flops 95000002560 | bytes 200000000 | tf_op jit(solution)/shard_map/layers/pallas_call | solution.py:439
  396.8 2.1 copy.10
Async XLA Ops:
  20.6 3.4 slice-start
  20.6 3.4 copy-start

commit v2 on v0

v2 whole, which is shorter than its diff:
```python
import jax
import jax.numpy as jnp
from jax import lax
from jax.experimental import pallas as pl
from jax.experimental.pallas import tpu as pltpu
from jax.sharding import PartitionSpec as P

EPS = 1e-6
NEG_BIG = -1e30
MESH = pl.DeviceIdType.MESH
TILE = 512
RELS = (0, -1, 1, 2)
KINDS = ('i0', 'i1', 'o')
GROUPS = tuple((layer, kind) for layer in (0, 1) for kind in KINDS)
F32 = jnp.float32
BF16 = jnp.bfloat16
ORDER = ((0, 1), (4, 8), (2, 3), (5, 9), (6, 10), (7, 11), (12, 13), (14, 15))
N_EVENTS = 32
START_NEXT = 20
OFFSETS = (0, 1.5, 7.5, 13.5, 19.5, 32, 38, 47)
BEGINS = (15, 72, 117, 165, 215, 259)
PHASES = ((34, 43, 76, 120, (144, 155, 160)), (206, 214, 219, 263, (290, 300, 304)))
STEP = 1.5
SUB = 128
BLOCKS = ((0, 0), (1, 0), (-1, 0), (0, 1), (0, -1), (1, 1), (-1, -1), (1, -1),
          (-1, 1), (2, 0), (0, 2), (2, -1), (-1, 2), (1, 2), (2, 1), (2, 2))
CHUNKS = ((0, 8), (8, 12), (12, 16))
CHUNK_EVENTS = (20, 28, 32)


def aligned(value, n):
    return value if isinstance(value, int) else pl.multiple_of(value, n)


def dot(a, b):
    return jnp.dot(a, b, preferred_element_type=F32)


def layer_kernel(ring, x_ref, len_ref, gain_in, win_ref, wkv_ref, wout_ref, y_ref, wi0, wi1, woutb,
                 gain_ref, h_all, joined, kvx, qb, wt, wo, zp, zrp, xh, xf, zs, hid, gbuf,
                 gsend, grecv, wsend, wrecv, asend, arecv, rsend, rrecv, bsem, tsem, osem):
    batch, blk, width = x_ref.shape
    shard = win_ref.shape[1]
    out_rows = wout_ref.shape[1]
    head = qb.shape[-1]
    kvc = kvx.shape[-1]
    seq = h_all.shape[1]
    n_data = gbuf.shape[0]
    ff = out_rows - head
    half_ff = ff // 2
    me = lax.axis_index('data')
    mi = lax.axis_index('model')
    yy = lax.rem(me, ring)
    zz = lax.div(me, ring)
    xx = lax.div(mi, 2)
    cc = lax.rem(mi, 2)

    def wrap(value, rel):
        return lax.rem(value + (rel + ring), ring)

    def data_at(ry, rz):
        return wrap(zz, rz) * ring + wrap(yy, ry)

    def dev_data(ry, rz):
        return {'data': data_at(ry, rz), 'model': mi}

    def dev_x(rx):
        return {'data': me, 'model': wrap(xx, rx) * 2 + cc}

    partner = {'data': me, 'model': xx * 2 + (1 - cc)}

    barrier = pltpu.get_barrier_semaphore()
    for ry in range(ring):
        for rz in range(ring):
            if ry or rz:
                pl.semaphore_signal(barrier, inc=1, device_id=dev_data(ry, rz), device_id_type=MESH)
    for dev in (dev_x(1), dev_x(-1), partner):
        pl.semaphore_signal(barrier, inc=1, device_id=dev, device_id_type=MESH)

    my_rows = pl.ds(pl.multiple_of(me * shard, 128), shard)
    locals_ = []

    def local(layer, i, src, dst):
        locals_.append(pltpu.make_async_copy(src, dst, bsem.at[layer, i]))

    for layer in (0, 1):
        kv_cols = pl.ds(pl.multiple_of(xx * kvc, 128), kvc)
        local(layer, 0, wkv_ref.at[layer, :, kv_cols], wi0.at[layer, my_rows, pl.ds(0, kvc)])
        local(layer, 1, win_ref.at[layer, :, pl.ds(0, head + half_ff)], wi0.at[layer, my_rows, pl.ds(kvc, head + half_ff)])
        local(layer, 2, win_ref.at[layer, :, pl.ds(head + ff, half_ff)], wi0.at[layer, my_rows, pl.ds(kvc + head + half_ff, half_ff)])
        local(layer, 3, win_ref.at[layer, :, pl.ds(head + half_ff, half_ff)], wi1.at[layer, my_rows, pl.ds(0, half_ff)])
        local(layer, 4, win_ref.at[layer, :, pl.ds(head + ff + half_ff, half_ff)], wi1.at[layer, my_rows, pl.ds(half_ff, half_ff)])
        local(layer, 5, wout_ref.at[layer], woutb.at[layer, me])
    for copy in locals_:
        copy.start()
    gain_ref[0:gain_in.shape[0], :] = gain_in[...].astype(F32)
    gbuf[me] = gain_ref[...]
    hid[...] = x_ref[...]
    pl.semaphore_wait(barrier, n_data - 1 + 3)

    drains = []

    def remote(src, dst, ssem, rsem, dev):
        return pltpu.make_async_remote_copy(src_ref=src, dst_ref=dst, send_sem=ssem, recv_sem=rsem,
                                            device_id=dev, device_id_type=MESH)

    half_in = shard // 2
    half_out = out_rows // 2

    def unit(g, hf, rp, rq, part=None):
        layer, kind = GROUPS[g]
        s = data_at(rp, rq) if hf == 0 else data_at(rq, rp)
        if kind == 'o':
            n = half_out if part is None else half_out // 2
            return woutb.at[layer, s, pl.ds(hf * half_out + (0 if part is None else part * n), n), :]
        n = half_in if part is None else half_in // 2
        start = pl.multiple_of(s * shard + (hf * half_in + (0 if part is None else part * n)), 32)
        return (wi0 if kind == 'i0' else wi1).at[layer, pl.ds(start, n), :]

    def along(hf, primary, rel):
        on_y = (hf == 0) == primary
        return dev_data(rel, 0) if on_y else dev_data(0, rel)

    def send(g, hf, idx, rel, primary, to, part=None):
        def build():
            ref = unit(g, hf, rel[0], rel[1], part)
            return remote(ref, ref, wsend.at[g, hf, idx], wrecv.at[g, hf, idx], along(hf, primary, to))
        build().start()
        drains.append(build)

    def spec(idx):
        if idx < 4:
            return ((-1, 0, None), (1, 0, None), (2, 0, 0), (2, 0, 1))[idx]
        return (RELS[idx % 4], (None, -1, 1, 2)[idx // 4], None)

    def start_group(g):
        for hf in (0, 1):
            send(g, hf, 0, (0, 0), True, 1)
            send(g, hf, 1, (0, 0), True, -1)
        for hf in (0, 1):
            send(g, hf, 4, (0, 0), False, 1)
            send(g, hf, 8, (0, 0), False, -1)

    def arrive(g, hf, idx):
        rp, rq, part = spec(idx)
        ref = unit(g, hf, rp, rq, part)
        remote(ref, ref, wsend.at[g, hf, idx], wrecv.at[g, hf, idx], along(hf, True, 1)).wait_recv()
        if idx < 2:
            send(g, hf, idx + 2, (rp, rq), True, -rp, idx)
        elif idx == 3:
            send(g, hf, 7, (rp, rq), False, 1)
            send(g, hf, 11, (rp, rq), False, -1)
        elif idx in (4, 5):
            send(g, hf, idx + 8, (rp, rq), False, 1)
        elif idx in (10, 11):
            send(g, hf, idx + 4, (rp, rq), False, -1)

    def turn_neighbors(g):
        for hf in (0, 1):
            for at in (1, 2):
                send(g, hf, at + 4, (RELS[at], 0), False, 1)
                send(g, hf, at + 8, (RELS[at], 0), False, -1)

    sequence = [(hf, idx) for pair in ORDER for hf in (0, 1) for idx in pair]
    cursor = [0]

    def pump(n):
        for _ in range(n):
            g, k = divmod(cursor[0], N_EVENTS)
            if g < len(GROUPS):
                if k == START_NEXT and g + 1 < len(GROUPS):
                    start_group(g + 1)
                arrive(g, *sequence[k])
                if k == 3:
                    turn_neighbors(g)
                cursor[0] += 1

    def due(n):
        g, k = divmod(n, N_EVENTS)
        return BEGINS[g] + OFFSETS[k // 4]

    def pump_until(time):
        while cursor[0] < len(GROUPS) * N_EVENTS and due(cursor[0]) <= time:
            pump(1)

    def pump_to(g, n=N_EVENTS):
        pump(max(0, g * N_EVENTS + n - cursor[0]))

    gain_copies = []
    for ry in range(ring):
        for rz in range(ring):
            if ry or rz:
                k = rz * ring + ry
                remote(gain_ref, gbuf.at[me], gsend.at[k], grecv.at[k], dev_data(ry, rz)).start()
                gain_copies.append((k, ry, rz))
    for copy in locals_:
        copy.wait()
    start_group(0)
    for k, ry, rz in gain_copies:
        src = gbuf.at[data_at(-ry, -rz)]
        remote(gain_ref, src, gsend.at[k], grecv.at[k], partner).wait()

    class Gather:
        def __init__(self, layer, kind, block):
            self.layer, self.kind, self.block, self.sent = layer, kind, block, []

        def send(self, idx, place, to):
            def build():
                ref = self.block(*place)
                dev = partner if to == 0 else dev_x(to)
                return remote(ref, ref, asend.at[self.layer, self.kind, idx], arecv.at[self.layer, self.kind, idx], dev)
            build().start()
            self.sent.append(build)

        def wait(self, idx, ref):
            remote(ref, ref, asend.at[self.layer, self.kind, idx], arecv.at[self.layer, self.kind, idx], partner).wait_recv()

        def start(self):
            self.send(0, (0, cc), 1)
            self.send(1, (0, cc), -1)
            self.send(4, (0, cc), 0)

        def near(self):
            self.wait(0, self.block(-1, cc))
            self.send(2, (-1, cc, 0), 1)
            self.send(5, (-1, cc), 0)
            self.wait(1, self.block(1, cc))
            self.send(3, (1, cc, 1), -1)
            self.send(6, (1, cc), 0)

        def far(self):
            self.wait(2, self.block(2, cc, 0))
            self.send(7, (2, cc, 0), 0)
            self.wait(3, self.block(2, cc, 1))
            self.send(8, (2, cc, 1), 0)

        def rest(self):
            block = self.block
            self.wait(4, block(0, 1 - cc))
            self.wait(5, block(-1, 1 - cc))
            self.wait(6, block(1, 1 - cc))
            self.wait(7, block(2, 1 - cc, 0))
            self.wait(8, block(2, 1 - cc, 1))

        def drain(self):
            for build in self.sent:
                build().wait_send()

    def h_block(rx, core, part=None):
        rows = pl.ds(pl.multiple_of((wrap(xx, rx) * 2 + core) * blk, 32), blk)
        return h_all.at[:, rows, :] if part is None else h_all.at[part, rows, :]

    def kv_block(rx, core, part=None):
        ref = kvx.at[wrap(xx, rx), core]
        return ref if part is None else ref.at[pl.ds(part * (seq // 2), seq // 2), :]

    def norm(layer):
        rows = pl.ds(pl.multiple_of(mi * blk, 32), blk)
        for b in range(batch):
            values = hid[b].astype(F32)
            centered = values - jnp.mean(values, axis=-1, keepdims=True)
            var = jnp.mean(centered * centered, axis=-1, keepdims=True)
            normed = centered * lax.rsqrt(var + EPS)
            for i in range(n_data):
                cols = slice(i * shard, (i + 1) * shard)
                h_all[b, rows, cols] = (normed[:, cols] * gbuf[i, layer:layer + 1, :]).astype(BF16)

    m_rows = seq // 2
    half_tiles = half_ff // head

    class Tile:
        def __init__(self, src, slot, pieces):
            self.copies = []
            at = 0
            for i, (start, n) in enumerate(pieces):
                self.copies.append(pltpu.make_async_copy(src.at[:, pl.ds(start, n)], wt.at[slot, :, pl.ds(at, n)], tsem.at[slot, i]))
                at += n

        def start(self):
            for copy in self.copies:
                copy.start()

        def wait(self):
            for copy in self.copies:
                copy.wait()

    def mlp_tile(layer, part, t, slot):
        src = (wi0 if part == 0 else wi1).at[layer]
        first = aligned((kvc + head if part == 0 else 0) + t * head, 128)
        return Tile(src, slot, ((first, head), (aligned(first + half_ff, 128), head)))

    def over_rows(fn):
        def body(i, carry):
            b = lax.div(i, 2)
            rows = pl.ds(pl.multiple_of(lax.rem(i, 2) * m_rows, m_rows), m_rows)
            fn(b, rows)
            return carry
        lax.fori_loop(0, 2 * batch, body, 0)

    def mlp(layer, part, begin, slot0, extra):
        blocks = 2 * batch

        def body(step, carry):
            t = lax.div(step, blocks)
            i = lax.rem(step, blocks)
            b = lax.div(i, 2)
            slot = lax.rem(t + slot0, 2)

            @pl.when(i == 0)
            def _():
                mlp_tile(layer, part, t, slot).wait()

            cols = pl.ds(pl.multiple_of(head + part * half_ff + t * head, head), head)
            for sub in range(m_rows // SUB):
                at = pl.ds(pl.multiple_of(lax.rem(i, 2) * m_rows + sub * SUB, SUB), SUB)
                res = dot(h_all[b, at, :], wt[slot])
                gate = res[:, :head].astype(BF16).astype(F32)
                up = res[:, head:].astype(BF16).astype(F32)
                joined[b, at, cols] = (gate * jax.nn.sigmoid(gate) * up).astype(BF16)

            @pl.when((i == blocks - 1) & (t + 2 < half_tiles))
            def _():
                mlp_tile(layer, part, t + 2, slot).start()

            for k in range(half_tiles * blocks):
                @pl.when(step == k)
                def _():
                    if k in extra:
                        extra[k]()
                    pump_until(begin + STEP * (k + 1))
            return carry

        lax.fori_loop(0, half_tiles * blocks, body, 0)

    def in_first(layer, kv, begin):
        kvq = Tile(wi0.at[layer], 0, ((0, kvc + head),))
        kvq.start()
        mlp_tile(layer, 0, 0, 1).start()
        kvq.wait()

        def do_kv(i, carry):
            rows = pl.ds(pl.multiple_of(i * m_rows, m_rows), m_rows)
            kvx[xx, cc, rows, :] = dot(h_all[cc, rows, :], wt[0, :, :kvc]).astype(BF16)
            return carry

        def do_q(b, rows):
            qb[b, rows, :] = dot(h_all[b, rows, :], wt[0, :, kvc:kvc + head]).astype(BF16)

        lax.fori_loop(0, 2, do_kv, 0)
        kv.start()
        pump_until(begin + 1)
        over_rows(do_q)
        mlp_tile(layer, 0, 1, 0).start()
        pump_until(begin + 3)

        mlp(layer, 0, begin + 3, 1, {5: kv.near, 9: kv.far})
        kv.rest()

    def in_second(layer, begin, then):
        mlp_tile(layer, 1, 0, 0).start()
        mlp_tile(layer, 1, 1, 1).start()
        mlp(layer, 1, begin, 0, {13: then})

    def wo_load(layer, k):
        return [pltpu.make_async_copy(woutb.at[layer, data_at(*BLOCKS[i])], wo.at[:, pl.ds(i * shard, shard)], osem.at[i])
                for i in range(*CHUNKS[k])]

    q_rows = 256

    def attention():
        def body(b, carry):
            for m in range(seq // q_rows):
                keys = (m + 1) * q_rows
                q = qb[b, m * q_rows:(m + 1) * q_rows, :]
                k = jnp.concatenate([kvx[0, b, :keys, :], kvx[1, b, :keys, :]], axis=-1)
                v = jnp.concatenate([kvx[2, b, :keys, :], kvx[3, b, :keys, :]], axis=-1)
                s = lax.dot_general(q, k, (((1,), (1,)), ((), ())), preferred_element_type=F32) * head ** -0.5
                row = lax.broadcasted_iota(jnp.int32, (q_rows, keys), 0) + m * q_rows
                col = lax.broadcasted_iota(jnp.int32, (q_rows, keys), 1)
                allowed = (col <= row) & (col < len_ref[b])
                s = jnp.where(allowed, s, NEG_BIG)
                e = jnp.exp(s - jnp.max(s, axis=-1, keepdims=True))
                p = e / jnp.sum(e, axis=-1, keepdims=True)
                o = dot(p, v.astype(F32))
                joined[b, m * q_rows:(m + 1) * q_rows, :head] = o.astype(BF16)
            return carry
        lax.fori_loop(0, batch, body, 0)

    PAIRS = (2, 1, -1, 0)
    pair_rows = 2 * blk

    def chunk_ds(k):
        first, last = CHUNKS[k]
        return pl.ds(first * shard, (last - first) * shard)

    def over_cols(k, fn):
        first, last = CHUNKS[k]

        def body(n, carry):
            fn(pl.ds(pl.multiple_of(first * shard + n * TILE, TILE), TILE))
            return carry
        lax.fori_loop(0, (last - first) * shard // TILE, body, 0)

    def out_proj(k, p):
        rows = pl.ds(pl.multiple_of(wrap(xx, PAIRS[p]) * pair_rows, 64), pair_rows)

        def fn(cols):
            lhs = joined[:, rows, :].reshape(batch * pair_rows, out_rows)
            res = dot(lhs, wo[:, cols]).astype(BF16)
            zp[p, :, :, cols] = res.reshape(batch, pair_rows, TILE)
        over_cols(k, fn)

    mine_rows = pl.ds(pl.multiple_of(cc * blk, 32), blk)
    other_rows = pl.ds(pl.multiple_of((1 - cc) * blk, 32), blk)

    class Scatter:
        def __init__(self, layer, k, out_ref):
            self.layer, self.k, self.out_ref, self.sent = layer, k, out_ref, []

        def send(self, idx, src, dst, dev):
            copy = remote(src, dst, rsend.at[self.layer, self.k, idx], rrecv.at[self.layer, self.k, idx], dev)
            copy.start()
            self.sent.append(copy)

        def wait(self, idx, dst):
            remote(dst, dst, rsend.at[self.layer, self.k, idx], rrecv.at[self.layer, self.k, idx], partner).wait_recv()

        def begin(self, p):
            here = chunk_ds(self.k)
            self.send(p, zp.at[p, :, other_rows, here], zrp.at[p, :, :, here], partner)

        def finish(self, p):
            k = self.k
            here = chunk_ds(k)

            def base(p, b, cols):
                return zp[p, b, mine_rows, cols].astype(F32) + zrp[p, b, :, cols].astype(F32)

            self.wait(p, zrp.at[p, :, :, here])
            if p == 0:
                def fn(cols):
                    for b in range(batch):
                        zs[0, b, :, cols] = base(0, b, cols).astype(BF16)
                over_cols(k, fn)
                self.send(4, zs.at[0, 0, :, here], xh.at[0, :, here], dev_x(1))
                self.send(5, zs.at[0, 1, :, here], xh.at[1, :, here], dev_x(-1))
            elif p < 3:
                self.wait(3 + p, xh.at[p - 1, :, here])

                def fn(cols):
                    for b in range(batch):
                        total = base(p, b, cols)
                        if b == p - 1:
                            total = total + xh[p - 1, :, cols].astype(F32)
                        zs[p, b, :, cols] = total.astype(BF16)
                over_cols(k, fn)
                self.send(5 + p, zs.at[p, :, :, here], xf.at[p - 1, :, :, here], dev_x(1 if p == 1 else -1))
            else:
                self.wait(6, xf.at[0, :, :, here])
                self.wait(7, xf.at[1, :, :, here])
                for b in range(batch):
                    for i in range(*CHUNKS[k]):
                        cols = slice(i * shard, (i + 1) * shard)
                        total = base(3, b, cols) + xf[0, b, :, cols].astype(F32) + xf[1, b, :, cols].astype(F32)
                        place = pl.ds(pl.multiple_of(data_at(*BLOCKS[i]) * shard, shard), shard)
                        self.out_ref[b, :, place] = (hid[b, :, place].astype(F32) + total).astype(BF16)

    for layer in (0, 1):
        g = 3 * layer
        h = Gather(layer, 0, h_block)
        norm(layer)
        h.start()
        near, far, first, second, chunk_times = PHASES[layer]
        pump_until(near)
        h.near()
        pump_until(far)
        h.far()
        h.rest()
        pump_to(g)
        kv = Gather(layer, 1, kv_block)
        in_first(layer, kv, first)
        attention()
        pump_to(g + 1)
        loads = [wo_load(layer, k) for k in range(len(CHUNKS))]

        def load(k):
            pump_to(g + 2, CHUNK_EVENTS[k])
            for copy in wo_load(layer, k):
                copy.start()

        in_second(layer, second, lambda: load(0))
        h.drain()
        kv.drain()
        parts = [Scatter(layer, k, hid if layer == 0 else y_ref) for k in range(len(CHUNKS))]
        for k, part in enumerate(parts):
            for copy in loads[k]:
                copy.wait()
            for p in range(4):
                out_proj(k, p)
                part.begin(p)
                if p == 2 and k + 1 < len(CHUNKS):
                    load(k + 1)
                else:
                    pump_until(chunk_times[k] + 2 * (p + 1))
                if p:
                    part.finish(p - 1)
                if p == 2 and k:
                    parts[k - 1].finish(3)
        parts[-1].finish(3)
        for part in parts:
            for copy in part.sent:
                copy.wait_send()

    for build in drains:
        build().wait_send()


def solution(mesh):
    batch_spec = ('replica', 'data')
    model_size = mesh.shape['model']
    n_data = mesh.shape['data']
    ring = 4
    assert model_size == 2 * ring and n_data == ring * ring

    def device_body(x_in, lengths, norm_gain, w_in, w_kv, w_out):
        batch, blk, width = x_in.shape
        layers, shard, in_cols = w_in.shape
        out_rows = w_out.shape[1]
        head = w_kv.shape[-1] // 2
        seq = blk * model_size
        ff = out_rows - head
        kvc = 2 * head // ring
        vmem = pl.BlockSpec(memory_space=pltpu.VMEM)
        hbm = pl.BlockSpec(memory_space=pl.ANY)
        dma = pltpu.SemaphoreType.DMA
        groups = len(GROUPS)
        y = pl.pallas_call(
            lambda *refs: layer_kernel(ring, *refs),
            name='layers',
            out_shape=(
                jax.ShapeDtypeStruct(x_in.shape, BF16),
                jax.ShapeDtypeStruct((layers, width, kvc + head + ff), BF16),
                jax.ShapeDtypeStruct((layers, width, ff), BF16),
                jax.ShapeDtypeStruct((layers, n_data, out_rows, shard), BF16),
            ),
            in_specs=[vmem, pl.BlockSpec(memory_space=pltpu.SMEM)] + [vmem] * 4,
            out_specs=(vmem, hbm, hbm, hbm),
            scratch_shapes=[
                pltpu.VMEM((8, shard), F32),
                pltpu.VMEM((batch, seq, width), BF16),
                pltpu.VMEM((batch, seq, out_rows), BF16),
                pltpu.VMEM((ring, batch, seq, kvc), BF16),
                pltpu.VMEM((batch, seq, head), BF16),
                pltpu.VMEM((2, width, TILE), BF16),
                pltpu.VMEM((out_rows, width), BF16),
                pltpu.VMEM((4, batch, 2 * blk, width), BF16),
                pltpu.VMEM((4, batch, blk, width), BF16),
                pltpu.VMEM((2, blk, width), BF16),
                pltpu.VMEM((2, batch, blk, width), BF16),
                pltpu.VMEM((3, batch, blk, width), BF16),
                pltpu.VMEM((batch, blk, width), BF16),
                pltpu.VMEM((n_data, 8, shard), F32),
                dma((n_data,)), dma((n_data,)),
                dma((groups, 2, 16)), dma((groups, 2, 16)),
                dma((2, 2, 9)), dma((2, 2, 9)),
                dma((2, 3, 8)), dma((2, 3, 8)),
                dma((2, 6)), dma((2, 2)), dma((n_data,)),
            ],
            compiler_params=pltpu.CompilerParams(
                collective_id=0, has_side_effects=True, vmem_limit_bytes=67043328),
            cost_estimate=pl.CostEstimate(flops=90_000_000_000, bytes_accessed=200_000_000, transcendentals=0),
        )(x_in, lengths, norm_gain, w_in, w_kv, w_out)[0]
        return y

    in_specs = (P(batch_spec, 'model', None), P(batch_spec), P(None, 'data'), P(None, 'data', 'model'), P(None, 'data', None), P(None, 'model', 'data'))
    return jax.shard_map(device_body, mesh=mesh, in_specs=in_specs, out_specs=P(batch_spec, 'model', None), check_vma=False)
```

time: 725 us -> 365 us (0.50)
  waiting for transfers between devices: 511 us -> 0 us
  Pallas kernels: 0 us -> 363 us
  matrix products: 131 us -> 0 us
  blocking collectives: 39.4 us -> 0 us
  other arithmetic: 24.7 us -> 0 us
  between operations: 13.7 us -> 0.01 us
    all_gather x8 -> x0, waiting for transfers between devices: 442 us -> none  [the longest x2 222 us: device_body(): w_in_full = lax.all_gather(w_in[layer_idx], 'data', axis=0, tiled=True)]
    pallas_call x0 -> x1, Pallas kernels: none -> 363 us  [device_body(): pl.pallas_call(lambda *refs: layer_kernel(ring, *refs), name='layers', ou...]
    dot_general x10 -> x0, matrix products: 131 us -> none  [the longest x2 68.7 us: device_body(): jnp.einsum('btd,dc->btc', normed_all, w_in_full, preferred_element_type=j...]
    reduce_scatter x2 -> x0, waiting for transfers between devices: 66.6 us -> none  [device_body(): z_loc = lax.psum_scatter(part_z, 'model', scatter_dimension=1, tiled=True)]
    all_gather x2 -> x0, blocking collectives: 39.4 us -> none  [device_body(): gain_full = lax.all_gather(norm_gain[layer_idx], 'data', axis=0, tiled=True)]
    convert_element_type x7 -> x0, other arithmetic: 16.7 us -> none  [the longest x2 10.6 us: device_body(): mlp_out = (jax.nn.silu(gate_pre) * up_proj).astype(jnp.bfloat16)]
    reduce_sum x6 -> x0, other arithmetic: 7.72 us -> none  [the longest x2 2.98 us: device_body(): attn_prob = jax.nn.softmax(scores, axis=-1)]
  transfers between devices with their start and end apart: 10 -> 0, of which waited for: 10 -> 0; matrix products, arithmetic and copies ran while one was open for 16% -> 0% of each run, Pallas kernels for 0% -> 0%
where the time goes in v2:
time: 365 us
  Pallas kernels  363 us (99%)
    pallas_call x1, Pallas kernels, device_body(): pl.pallas_call(lambda *refs: layer_kernel(ring, *refs), name='layers', ou...  363 us

profile of v2, /device:TPU:1, one launch (start us, length us, event | category | flops | bytes accessed | tf_op | source)
XLA Modules:
  0.0 364.9 jit_solution(4654155160315195363)
XLA Ops:
  0.0 362.8 %layers.1 = (bf16[2,96,2048]{2,1,0:T(8,128)(2,1)}, bf16[2,2048,2432]{2,1,0:T(8,128)(2,1)}, bf16[2,2048,2048]{2,1,0:T(8,128)(2,1)}, bf16[2,16,2304,128]{3,2,1,0:T(8,128)(2,1)}) custom-call(bf16[2,96,2048]{2,1,0:T(8,128)(2,1)} %refs_0_.1, s32[2]{0:T(128)} %refs_1_.1, bf16[2,128]{1,0:T(2,128)(2,1)} %refs_2_.1, bf16[2,128,4352]{2,1,0:T(8,128)(2,1)} %refs_3_.1, ...), custom_call_target="tpu_custom_call" | custom-call | flops 89999998976 | bytes 200000000 | tf_op jit(solution)/shard_map/layers/pallas_call | solution.py:537
  362.8 2.1 copy.8

commit v3 on v2

--- a/solution.py
+++ b/solution.py
@@ -9,17 +9,20 @@
 NEG_BIG = -1e30
 MESH = pl.DeviceIdType.MESH
 TILE = 512
+BOTH = (0, 1)
 RELS = (0, -1, 1, 2)
 KINDS = ('i0', 'i1', 'o')
-GROUPS = tuple((layer, kind) for layer in (0, 1) for kind in KINDS)
+GROUPS = tuple((layer, kind) for layer in BOTH for kind in KINDS)
 F32 = jnp.float32
 BF16 = jnp.bfloat16
 ORDER = ((0, 1), (4, 8), (2, 3), (5, 9), (6, 10), (7, 11), (12, 13), (14, 15))
 N_EVENTS = 32
-START_NEXT = 20
+START_NEXT = 14
+EARLY = 8
+SHIFT = 10
 OFFSETS = (0, 1.5, 7.5, 13.5, 19.5, 32, 38, 47)
 BEGINS = (15, 72, 117, 165, 215, 259)
-PHASES = ((34, 43, 76, 120, (144, 155, 160)), (206, 214, 219, 263, (290, 300, 304)))
+PHASES = ((34, 43, 74, 118, (140, 168, 174)), (203, 211, 217, 261, (283, 294, 304)))
 STEP = 1.5
 SUB = 128
 BLOCKS = ((0, 0), (1, 0), (-1, 0), (0, 1), (0, -1), (1, 1), (-1, -1), (1, -1),
@@ -83,7 +86,7 @@
     def local(layer, i, src, dst):
         locals_.append(pltpu.make_async_copy(src, dst, bsem.at[layer, i]))
 
-    for layer in (0, 1):
+    for layer in BOTH:
         kv_cols = pl.ds(pl.multiple_of(xx * kvc, 128), kvc)
         local(layer, 0, wkv_ref.at[layer, :, kv_cols], wi0.at[layer, my_rows, pl.ds(0, kvc)])
         local(layer, 1, win_ref.at[layer, :, pl.ds(0, head + half_ff)], wi0.at[layer, my_rows, pl.ds(kvc, head + half_ff)])
@@ -134,10 +137,10 @@
         return (RELS[idx % 4], (None, -1, 1, 2)[idx // 4], None)
 
     def start_group(g):
-        for hf in (0, 1):
+        for hf in BOTH:
             send(g, hf, 0, (0, 0), True, 1)
             send(g, hf, 1, (0, 0), True, -1)
-        for hf in (0, 1):
+        for hf in BOTH:
             send(g, hf, 4, (0, 0), False, 1)
             send(g, hf, 8, (0, 0), False, -1)
 
@@ -156,35 +159,35 @@
             send(g, hf, idx + 4, (rp, rq), False, -1)
 
     def turn_neighbors(g):
-        for hf in (0, 1):
+        for hf in BOTH:
             for at in (1, 2):
                 send(g, hf, at + 4, (RELS[at], 0), False, 1)
                 send(g, hf, at + 8, (RELS[at], 0), False, -1)
 
-    sequence = [(hf, idx) for pair in ORDER for hf in (0, 1) for idx in pair]
+    sequence = [(hf, idx) for pair in ORDER for hf in BOTH for idx in pair]
+    order = sorted(((g, k) for g in range(len(GROUPS)) for k in range(N_EVENTS)),
+                   key=lambda e: e[0] * N_EVENTS + e[1] - (SHIFT if e[1] < EARLY and e[0] else 0))
     cursor = [0]
 
     def pump(n):
         for _ in range(n):
+            g, k = order[cursor[0]]
+            if k == START_NEXT and g + 1 < len(GROUPS):
+                start_group(g + 1)
+            arrive(g, *sequence[k])
+            if k == 3:
+                turn_neighbors(g)
+            cursor[0] += 1
+
+    def pump_until(time):
+        while cursor[0] < len(order):
             g, k = divmod(cursor[0], N_EVENTS)
-            if g < len(GROUPS):
-                if k == START_NEXT and g + 1 < len(GROUPS):
-                    start_group(g + 1)
-                arrive(g, *sequence[k])
-                if k == 3:
-                    turn_neighbors(g)
-                cursor[0] += 1
-
-    def due(n):
-        g, k = divmod(n, N_EVENTS)
-        return BEGINS[g] + OFFSETS[k // 4]
-
-    def pump_until(time):
-        while cursor[0] < len(GROUPS) * N_EVENTS and due(cursor[0]) <= time:
+            if BEGINS[g] + OFFSETS[k // 4] > time:
+                break
             pump(1)
 
     def pump_to(g, n=N_EVENTS):
-        pump(max(0, g * N_EVENTS + n - cursor[0]))
+        pump(max(0, order.index((g, n - 1)) + 1 - cursor[0]))
 
     gain_copies = []
     for ry in range(ring):
@@ -465,7 +468,7 @@
                         place = pl.ds(pl.multiple_of(data_at(*BLOCKS[i]) * shard, shard), shard)
                         self.out_ref[b, :, place] = (hid[b, :, place].astype(F32) + total).astype(BF16)
 
-    for layer in (0, 1):
+    for layer in BOTH:
         g = 3 * layer
         h = Gather(layer, 0, h_block)
         norm(layer)
@@ -498,14 +501,15 @@
             for p in range(4):
                 out_proj(k, p)
                 part.begin(p)
-                if p == 2 and k + 1 < len(CHUNKS):
-                    load(k + 1)
-                else:
-                    pump_until(chunk_times[k] + 2 * (p + 1))
+                pump_until(chunk_times[k] + p)
                 if p:
                     part.finish(p - 1)
                 if p == 2 and k:
                     parts[k - 1].finish(3)
+            if part is not parts[-1]:
+                load(k + 1)
+            else:
+                pump_until(chunk_times[k] + 6)
         parts[-1].finish(3)
         for part in parts:
             for copy in part.sent:

time: 365 us -> 340 us (0.932)
  Pallas kernels: 363 us -> 337 us
    pallas_call x1, Pallas kernels: 363 us -> 337 us  [device_body(): pl.pallas_call(lambda *refs: layer_kernel(ring, *refs), name='layers', ou...]
where the time goes in v3:
time: 340 us; the launch traced here: 339 us
  Pallas kernels  337 us (99%)
    pallas_call x1, Pallas kernels, device_body(): pl.pallas_call(lambda *refs: layer_kernel(ring, *refs), name='layers', ou...  337 us

profile of v3, /device:TPU:1, one launch (start us, length us, event | category | flops | bytes accessed | tf_op | source)
XLA Modules:
  0.0 338.8 jit_solution(16906875388570983105)
XLA Ops:
  0.0 336.7 %layers.1 = (bf16[2,96,2048]{2,1,0:T(8,128)(2,1)}, bf16[2,2048,2432]{2,1,0:T(8,128)(2,1)}, bf16[2,2048,2048]{2,1,0:T(8,128)(2,1)}, bf16[2,16,2304,128]{3,2,1,0:T(8,128)(2,1)}) custom-call(bf16[2,96,2048]{2,1,0:T(8,128)(2,1)} %refs_0_.1, s32[2]{0:T(128)} %refs_1_.1, bf16[2,128]{1,0:T(2,128)(2,1)} %refs_2_.1, bf16[2,128,4352]{2,1,0:T(8,128)(2,1)} %refs_3_.1, ...), custom_call_target="tpu_custom_call" | custom-call | flops 89999998976 | bytes 200000000 | tf_op jit(solution)/shard_map/layers/pallas_call | solution.py:541
  336.7 2.1 copy.8

commit v4 on v3

--- a/solution.py
+++ b/solution.py
@@ -22,8 +22,9 @@
 SHIFT = 10
 OFFSETS = (0, 1.5, 7.5, 13.5, 19.5, 32, 38, 47)
 BEGINS = (15, 72, 117, 165, 215, 259)
-PHASES = ((34, 43, 74, 118, (140, 168, 174)), (203, 211, 217, 261, (283, 294, 304)))
+PHASES = ((34, 43, 74, 118, (140, 168, 174)), (204, 216, 219, 261, (283, 294, 304)))
 STEP = 1.5
+LAGS = (2, 5, 5, 8)
 SUB = 128
 BLOCKS = ((0, 0), (1, 0), (-1, 0), (0, 1), (0, -1), (1, 1), (-1, -1), (1, -1),
           (-1, 1), (2, 0), (0, 2), (2, -1), (-1, 2), (1, 2), (2, 1), (2, 2))
@@ -495,6 +496,15 @@
         h.drain()
         kv.drain()
         parts = [Scatter(layer, k, hid if layer == 0 else y_ref) for k in range(len(CHUNKS))]
+        pending = []
+        step = 0
+
+        def settle(upto):
+            for entry in sorted(pending):
+                if entry[0] <= upto:
+                    pending.remove(entry)
+                    parts[entry[1]].finish(entry[2])
+
         for k, part in enumerate(parts):
             for copy in loads[k]:
                 copy.wait()
@@ -502,15 +512,16 @@
                 out_proj(k, p)
                 part.begin(p)
                 pump_until(chunk_times[k] + p)
-                if p:
-                    part.finish(p - 1)
-                if p == 2 and k:
-                    parts[k - 1].finish(3)
+                pending.append((step + LAGS[p], k, p))
+                step += 1
+                settle(step)
             if part is not parts[-1]:
+                if layer + k == 0:
+                    settle(len(order))
                 load(k + 1)
             else:
                 pump_until(chunk_times[k] + 6)
-        parts[-1].finish(3)
+        settle(len(order))
         for part in parts:
             for copy in part.sent:
                 copy.wait_send()

time: 340 us -> 329 us (0.968)
  Pallas kernels: 337 us -> 325 us
    pallas_call x1, Pallas kernels: 337 us -> 325 us  [device_body(): pl.pallas_call(lambda *refs: layer_kernel(ring, *refs), name='layers', ou...]
where the time goes in v4:
time: 329 us; the launch traced here: 327 us
  Pallas kernels  325 us (99%)
    pallas_call x1, Pallas kernels, device_body(): pl.pallas_call(lambda *refs: layer_kernel(ring, *refs), name='layers', ou...  325 us

profile of v4, /device:TPU:1, one launch (start us, length us, event | category | flops | bytes accessed | tf_op | source)
XLA Modules:
  0.0 327.3 jit_solution(4889410427400175860)
XLA Ops:
  0.0 325.2 %layers.1 = (bf16[2,96,2048]{2,1,0:T(8,128)(2,1)}, bf16[2,2048,2432]{2,1,0:T(8,128)(2,1)}, bf16[2,2048,2048]{2,1,0:T(8,128)(2,1)}, bf16[2,16,2304,128]{3,2,1,0:T(8,128)(2,1)}) custom-call(bf16[2,96,2048]{2,1,0:T(8,128)(2,1)} %refs_0_.1, s32[2]{0:T(128)} %refs_1_.1, bf16[2,128]{1,0:T(2,128)(2,1)} %refs_2_.1, bf16[2,128,4352]{2,1,0:T(8,128)(2,1)} %refs_3_.1, ...), custom_call_target="tpu_custom_call" | custom-call | flops 89999998976 | bytes 200000000 | tf_op jit(solution)/shard_map/layers/pallas_call | solution.py:552
  325.2 2.1 copy.8
